TPU v7x, 32 devices: a whole 2x2x4 slice. The times are simulated.
32 devices in a mesh: grp: 2 (over x), tile: 16 (over z, y, core).
Axes of the slice: x: 2, y: 2, z: 4, core: 2. Of those that a mesh axis runs over, the one named last changes fastest.
Arguments:
- visibility: bfloat16 [2, 512, 512, 1024], P(None, 'tile', None, 'grp'), may hold values from -3 to 3, as said below
- dish_pair_okay: int32 [512, 512], P('tile'), may hold values 0 or 1
- triangles: int32 [3, 32768], P(None, 'tile'), may hold values from 0 to 511, as said below
Outputs:
- triangle_means: float32 [2, 32768], P(None, 'tile')
- closure_spectrum: float32 [2, 1024], P(None, ('grp', 'tile'))
Inputs may be any that keep to these rules, and one draw needn't show every extreme that they name: Both parts of every visibility lie in -3 to 3. `triangles`: column j belongs to block d = j // 2048 and level k = (j % 2048) // 1024; its first antenna lies in block d (antennas d * 32 to d * 32 + 31), its second in block d XOR 2**k, and its third is any antenna other than the first two.
All inputs are finite; a program needn't handle non-finite values. No bound on the sum of `dish_pair_okay` on one device may be relied on, other than what follows from the above.
Results may differ from a plain program's by a relative error of at most 0.0003.
Values may be sent and summed in bfloat16 or wider, within the bound.
A program may use at most 128 MiB of HBM per device.

v0:
```python
import functools

import jax
import jax.numpy as jnp
from jax import lax
from jax.experimental import pallas as pl
from jax.experimental.pallas import tpu as pltpu
from jax.sharding import PartitionSpec as P

TRI_LVL = 1024
LANES = 128
SIDE = 256
FAR = 128
MESH = pl.DeviceIdType.MESH


def dot(a, b):
    return lax.dot_general(a, b, (((1,), (0,)), ((), ())), preferred_element_type=jnp.float32)


def fold(x):
    total = x[:8]
    for i in range(1, x.shape[0] // 8):
        total = total + x[i * 8 : i * 8 + 8]
    return total


def mega_kernel(
    vis,
    okay,
    tri,
    means,
    closure,
    table,
    ring,
    spread,
    gather,
    asked,
    got,
    ask_rows,
    own_rows,
    ask_smem,
    own_smem,
    bc_send,
    bc_recv,
    pair,
    prod,
    line,
    sums,
    spec_acc,
    spec_out,
    spec_recv,
    ring_sem,
    move_sem,
    idx_send,
    idx_recv,
    near_send,
    near_recv,
    far_send,
    far_recv,
    sum_send,
    sum_recv,
    spec_send_sem,
    spec_recv_sem,
    *,
    groups,
    tiles,
    levels,
    step_rows,
):
    _, dishes, cols, channels = vis.shape
    chunks = channels // LANES
    kinds = 2 * chunks
    block = SIDE // kinds
    blank = dishes * cols
    count = tri.shape[1] // levels
    packs = count // LANES
    last = levels - 1
    slots = ring.shape[0]
    steps = dishes // step_rows
    pieces = count // FAR
    width = channels // tiles
    me_g, me = lax.axis_index("grp"), lax.axis_index("tile")
    peers = [(lax.rem(me_g + k, groups), me) for k in range(1, groups)]
    others = [(me_g, lax.rem(me + k, tiles)) for k in range(1, tiles)]
    partner = [(me_g, jnp.bitwise_xor(me, 1 << level)) for level in range(levels)]

    barrier = pltpu.get_barrier_semaphore()
    for device in peers + others:
        pl.semaphore_signal(barrier, inc=1, device_id=device, device_id_type=MESH)

    def fetch(s, slot):
        return pltpu.make_async_copy(vis.at[:, pl.ds(s * step_rows, step_rows)], ring.at[slot], ring_sem.at[slot])

    for s in range(slots - 1):
        fetch(s, s).start()

    def remote(src, dst, send, recv, device):
        return pltpu.make_async_remote_copy(
            src_ref=src, dst_ref=dst, send_sem=send, recv_sem=recv, device_id=device, device_id_type=MESH
        )

    out_at = lax.broadcasted_iota(jnp.int32, (SIDE, SIDE), 0)
    in_at = lax.broadcasted_iota(jnp.int32, (SIDE, SIDE), 1)
    one, nil = jnp.ones((), jnp.float32), jnp.zeros((), jnp.float32)
    spread[...] = jnp.where(in_at == lax.rem(out_at, kinds) * block + out_at // kinds, one, nil).astype(spread.dtype)
    gather[...] = jnp.where(in_at == lax.rem(out_at, block) * kinds + out_at // block, one, nil).astype(gather.dtype)
    table[blank] = jnp.zeros((kinds, LANES), table.dtype)
    spec_acc[...] = jnp.zeros(spec_acc.shape, spec_acc.dtype)

    flags = okay[...].astype(jnp.float32).astype(jnp.bfloat16)

    def look_up(first, seconds):
        n = first.shape[1]
        hot = jnp.where(lax.broadcasted_iota(jnp.int32, (dishes, n), 0) == first, one, nil).astype(jnp.bfloat16)
        rows = lax.dot_general(flags, hot, (((0,), (0,)), ((), ())), preferred_element_type=jnp.float32)
        at = lax.broadcasted_iota(jnp.int32, (cols, n), 0)
        good = None
        for second in seconds:
            hit = jnp.sum(jnp.where(at == second, rows, 0.0), 0, keepdims=True)
            good = hit if good is None else good * hit
        return good

    for level in range(levels):
        for i in range(packs):
            at = level * count + i * LANES
            a, b, c = [tri[pl.ds(e, 1), pl.ds(at, LANES)] for e in range(3)]
            first = a - me * dishes
            second = b - jnp.bitwise_xor(me, 1 << level) * dishes
            good = look_up(first, (b, c)) > 0.5
            asked[level, pl.ds(i, 1), :] = jnp.clip(jnp.where(good, second * cols + c, blank), 0, blank)
            own_rows[level, 0, pl.ds(i, 1), :] = jnp.clip(first * cols + b, 0, blank)
            own_rows[level, 1, pl.ds(i, 1), :] = jnp.clip(first * cols + c, 0, blank)

    def turn(s):
        slot = lax.rem(s, slots)
        fetch(s, slot).wait()
        for a in range(step_rows):
            for u in range(cols // (2 * block)):
                base = u * 2 * block
                x = jnp.concatenate(
                    [
                        jnp.concatenate(
                            [
                                ring[slot, plane, a, pl.ds(base + g * block, block), pl.ds(c * LANES, LANES)]
                                for c in range(chunks)
                                for plane in range(2)
                            ],
                            0,
                        )
                        for g in range(2)
                    ],
                    1,
                )
                y = dot(spread[...], x)
                for g in range(2):
                    rows = y[:, g * LANES : (g + 1) * LANES].reshape(block, kinds, LANES)
                    table[pl.ds((s * step_rows + a) * cols + base + g * block, block)] = rows.astype(table.dtype)

    def turn_step(s, _):
        @pl.when(s + slots - 1 < steps)
        def _():
            fetch(s + slots - 1, lax.rem(s + slots - 1, slots)).start()

        turn(s)
        return 0

    lax.fori_loop(0, 1, turn_step, 0)
    pl.semaphore_wait(barrier, len(peers) + len(others))
    ask = [
        remote(asked.at[level], got.at[level], idx_send.at[level], idx_recv.at[level], partner[level])
        for level in range(levels)
    ]
    for copy in ask:
        copy.start()
    lax.fori_loop(1, steps, turn_step, 0)

    move_own = pltpu.make_async_copy(own_rows, own_smem, move_sem.at[levels])
    move_own.start()
    moves = []
    for level in reversed(range(levels)):
        ask[level].wait()
        for i in range(packs):
            row = got[level, pl.ds(i, 1), :]
            first, second = row // cols, lax.rem(row, cols)
            good = look_up(first, (second,)) > 0.5
            ask_rows[level, pl.ds(i, 1), :] = jnp.clip(jnp.where(good, row, blank), 0, blank)
        move = pltpu.make_async_copy(ask_rows.at[level], ask_smem.at[level], move_sem.at[level])
        move.start()
        moves.append(move)

    def take(level, start, n):
        unroll = 32

        def some(it, _):
            for u in range(unroll):
                j = start + it * unroll + u
                bc_send[level, j] = table[ask_smem[level, j // LANES, lax.rem(j, LANES)]]
            return 0

        lax.fori_loop(0, n // unroll, some, 0)

    far = [
        remote(
            bc_send.at[last, pl.ds(k * FAR, FAR)],
            bc_recv.at[last, pl.ds(k * FAR, FAR)],
            far_send.at[k],
            far_recv.at[k],
            partner[last],
        )
        for k in range(pieces)
    ]
    moves[0].wait()
    for k in range(pieces):
        take(last, k * FAR, FAR)
        if k > 0:
            far[k - 1].start()
    near = [
        remote(bc_send.at[level], bc_recv.at[level], near_send.at[level], near_recv.at[level], partner[level])
        for level in range(last)
    ]
    for move in moves[1:]:
        move.wait()
    for level in range(last):
        take(level, 0, count)
        if level == 0:
            far[pieces - 1].start()
    move_own.wait()
    for copy in near:
        copy.start()

    def products(level, n_blocks):
        def some(it, _):
            for s in range(n_blocks):
                start = (it * n_blocks + s) * block
                for u in range(block):
                    j = start + u
                    for e in range(2):
                        row = table[own_smem[level, e, j // LANES, lax.rem(j, LANES)]]
                        pair[s, e, pl.ds(u * kinds, kinds), :] = row
            for s in range(n_blocks):
                start = pl.multiple_of((it * n_blocks + s) * block, block)
                y = dot(gather[...], jnp.concatenate([pair[s, 0], pair[s, 1]], 1))
                for c in range(chunks):
                    at = 2 * c * block
                    a_r, a_i = y[at : at + block, :LANES], y[at + block : at + 2 * block, :LANES]
                    c_r, c_i = y[at : at + block, LANES:], y[at + block : at + 2 * block, LANES:]
                    prod[level, 0, c, pl.ds(start, block), :] = a_r * c_r + a_i * c_i
                    prod[level, 1, c, pl.ds(start, block), :] = a_i * c_r - a_r * c_i
            return 0

        lax.fori_loop(0, count // (n_blocks * block), some, 0)

    def bispectra(level, start, n):
        wide = min(2, n // block)
        acc = [None] * (3 * chunks)
        for s in range(n // (wide * block)):
            begin = pl.multiple_of(start + s * wide * block, wide * block)
            x = [bc_recv[level, pl.ds(begin + g * block, block)].reshape(SIDE, LANES) for g in range(wide)]
            y = dot(gather[...], jnp.concatenate(x, 1) if wide > 1 else x[0])
            for g in range(wide):
                lanes = slice(g * LANES, (g + 1) * LANES)
                rows = pl.ds(begin + g * block, block)
                total_r = total_i = None
                for c in range(chunks):
                    at = 2 * c * block
                    b_r, b_i = y[at : at + block, lanes], y[at + block : at + 2 * block, lanes]
                    w_r, w_i = prod[level, 0, c, rows, :], prod[level, 1, c, rows, :]
                    real = w_r * b_r - w_i * b_i
                    imag = w_r * b_i + w_i * b_r
                    norm = jnp.sqrt(real * real + imag * imag)
                    for part, value in enumerate((real, imag, norm)):
                        value = fold(value)
                        old = acc[3 * c + part]
                        acc[3 * c + part] = value if old is None else old + value
                    total_r = real if c == 0 else total_r + real
                    total_i = imag if c == 0 else total_i + imag
                line[0, pl.ds(s * wide * block + g * block, block), :] = total_r
                line[1, pl.ds(s * wide * block + g * block, block), :] = total_i
        for c in range(chunks):
            for part in range(3):
                spec_acc[c, part] = spec_acc[c, part] + acc[3 * c + part]
        ones = jnp.ones((8, LANES), jnp.float32)
        for part in range(2):
            lane_sum = lax.dot_general(
                ones,
                line[part, pl.ds(0, n), :],
                (((1,), (1,)), ((), ())),
                precision=lax.Precision.HIGHEST,
                preferred_element_type=jnp.float32,
            )
            sums[0, level, pl.ds(part, 1), pl.ds(pl.multiple_of(start, LANES), n)] = lane_sum[:1]

    products(0, 4 * 32 // block)
    for level in range(1, levels):
        products(level, 4 * 32 // block)
    for level in range(last):
        near[level].wait()
        lax.fori_loop(0, count // 256, lambda it, _, level=level: (bispectra(level, it * 256, 256), 0)[1], 0)
    early = [
        remote(sums.at[0, level], sums.at[k, level], sum_send.at[k, level], sum_recv.at[k, level], device)
        for k, device in enumerate(peers, 1)
        for level in range(last)
    ]
    for k in range(pieces):
        far[k].wait()
        bispectra(last, k * FAR, FAR)
        if k == 0:
            for copy in early:
                copy.start()
    copies = list(early)
    for k, device in enumerate(peers, 1):
        copies.append(remote(sums.at[0, last], sums.at[k, last], sum_send.at[k, last], sum_recv.at[k, last], device))
        copies[-1].start()
    for c in range(chunks):
        for part in range(3):
            spec_out[c, pl.ds(part, 1), :] = jnp.sum(spec_acc[c, part], 0, keepdims=True)
    spread_out = []
    for k, device in enumerate(others, 1):
        spread_out.append(
            remote(
                spec_out.at[device[1] * width // LANES],
                spec_recv.at[k],
                spec_send_sem.at[k],
                spec_recv_sem.at[k],
                device,
            )
        )
        spread_out[-1].start()
    for copy in copies:
        copy.wait()
    bands = channels * groups
    for level in range(levels):
        total = sums[0, level]
        for k in range(1, groups):
            total = total + sums[k, level]
        means[:, pl.ds(level * count, count)] = total / bands
    for copy in spread_out:
        copy.wait()
    total = spec_out[me * width // LANES]
    for k in range(1, tiles):
        total = total + spec_recv[k]
    closure[...] = total[:2] / (1.0 + total[2:3])


def body(visibility, dish_pair_okay, triangles):
    _, dishes, cols, channels = visibility.shape
    levels = triangles.shape[1] // TRI_LVL
    tiles, groups = lax.axis_size("tile"), lax.axis_size("grp")
    chunks = channels // LANES
    kinds = 2 * chunks
    packs = TRI_LVL // LANES
    step_rows, slots = 4, 3
    pieces = TRI_LVL // FAR
    width = channels // tiles
    vmem = pl.BlockSpec(memory_space=pltpu.VMEM)
    f32, bf16, i32 = jnp.float32, jnp.bfloat16, jnp.int32
    dma = pltpu.SemaphoreType.DMA
    triangle_means, closure = pl.pallas_call(
        functools.partial(mega_kernel, groups=groups, tiles=tiles, levels=levels, step_rows=step_rows),
        in_specs=[pl.BlockSpec(memory_space=pl.ANY), vmem, vmem],
        out_specs=[vmem, vmem],
        out_shape=[
            jax.ShapeDtypeStruct((2, triangles.shape[1]), f32),
            jax.ShapeDtypeStruct((2, LANES), f32),
        ],
        scratch_shapes=[
            pltpu.VMEM((dishes * cols + 1, kinds, LANES), bf16),
            pltpu.VMEM((slots, 2, step_rows, cols, channels), bf16),
            pltpu.VMEM((SIDE, SIDE), bf16),
            pltpu.VMEM((SIDE, SIDE), bf16),
            pltpu.VMEM((levels, packs, LANES), i32),
            pltpu.VMEM((levels, packs, LANES), i32),
            pltpu.VMEM((levels, packs, LANES), i32),
            pltpu.VMEM((levels, 2, packs, LANES), i32),
            pltpu.SMEM((levels, packs, LANES), i32),
            pltpu.SMEM((levels, 2, packs, LANES), i32),
            pltpu.VMEM((levels, TRI_LVL, kinds, LANES), bf16),
            pltpu.VMEM((levels, TRI_LVL, kinds, LANES), bf16),
            pltpu.VMEM((4, 2, SIDE, LANES), bf16),
            pltpu.VMEM((levels, 2, chunks, TRI_LVL, LANES), f32),
            pltpu.VMEM((2, 256, LANES), f32),
            pltpu.VMEM((groups, levels, 2, TRI_LVL), f32),
            pltpu.VMEM((chunks, 3, 8, LANES), f32),
            pltpu.VMEM((chunks, 8, LANES), f32),
            pltpu.VMEM((tiles, 8, LANES), f32),
            dma((slots,)),
            dma((levels + 1,)),
            dma((levels,)),
            dma((levels,)),
            dma((levels,)),
            dma((levels,)),
            dma((pieces,)),
            dma((pieces,)),
            dma((groups, levels)),
            dma((groups, levels)),
            dma((tiles,)),
            dma((tiles,)),
        ],
        compiler_params=pltpu.CompilerParams(
            collective_id=0, has_side_effects=True, vmem_limit_bytes=67043328
        ),
        name="bispectra",
    )(visibility, dish_pair_okay, triangles)
    at = lax.rem(lax.axis_index("tile") * width, LANES)
    return (triangle_means, lax.dynamic_slice_in_dim(closure, at, width, 1))


def solution(mesh):
    return jax.shard_map(
        body,
        mesh=mesh,
        in_specs=(P(None, "tile", None, "grp"), P("tile", None), P(None, "tile")),
        out_specs=(P(None, "tile"), P(None, ("grp", "tile"))),
        check_vma=False,
    )
```

profile of v0, /device:TPU:0, one launch (start us, length us, event | category | flops | bytes accessed | tf_op | source)
XLA Modules:
  0.0 75.6 jit_solution(16021257307763356191)
XLA Ops:
  0.6 72.4 %bispectra.1 = (f32[2,2048]{1,0:T(2,128)}, f32[2,128]{1,0:T(2,128)}) custom-call(bf16[2,32,512,512]{3,2,1,0:T(8,128)(2,1)} %vis.1, s32[32,512]{1,0:T(8,128)} %okay.1, s32[3,2048]{1,0:T(4,128)} %tri.1), custom_call_target="tpu_custom_call" | custom-call | tf_op jit(solution)/shard_map/bispectra/pallas_call | solution.py:359
  73.0 1.3 %constant_dynamic-slice_fusion = f32[2,32]{1,0:T(2,128)} fusion(f32[2,128]{1,0:T(2,128)} %get-tuple-element.5, s32[]{:T(128)S(6)} %select_n.3), kind=kLoop, calls=%fused_computation | loop fusion | bytes 516 | tf_op jit(solution)/shard_map/dynamic_slice | solution.py:406
  74.3 1.3 %copy.6 = f32[2,2048]{1,0:T(2,128)} copy(f32[2,2048]{1,0:T(2,128)} %get-tuple-element.8) | data formatting | bytes 32768
where the time goes:
time: 75.9 us; the launch traced here: 75.6 us
  Pallas kernels  72.4 us (95%)
  local copies, waits for them, and re-layouts  2.61 us (3%)
    pallas_call x1, Pallas kernels, body(): pl.pallas_call(functools.partial(mega_kernel, groups=groups, tiles=tiles,...  72.4 us

commit v1 on v0

--- a/solution.py
+++ b/solution.py
@@ -23,6 +23,10 @@
     for i in range(1, x.shape[0] // 8):
         total = total + x[i * 8 : i * 8 + 8]
     return total
+
+
+def far_room(count):
+    return count * 3 // 4 // FAR * FAR
 
 
 def mega_kernel(
@@ -37,7 +41,11 @@
     gather,
     asked,
     got,
-    ask_rows,
+    good_out,
+    good_in,
+    far_rows,
+    hot,
+    excess,
     own_rows,
     ask_smem,
     own_smem,
@@ -54,6 +62,8 @@
     move_sem,
     idx_send,
     idx_recv,
+    good_send,
+    good_recv,
     near_send,
     near_recv,
     far_send,
@@ -78,7 +88,8 @@
     last = levels - 1
     slots = ring.shape[0]
     steps = dishes // step_rows
-    pieces = count // FAR
+    room = far_room(count)
+    pieces = room // FAR
     width = channels // tiles
     me_g, me = lax.axis_index("grp"), lax.axis_index("tile")
     peers = [(lax.rem(me_g + k, groups), me) for k in range(1, groups)]
@@ -125,12 +136,11 @@
         for i in range(packs):
             at = level * count + i * LANES
             a, b, c = [tri[pl.ds(e, 1), pl.ds(at, LANES)] for e in range(3)]
-            first = a - me * dishes
             second = b - jnp.bitwise_xor(me, 1 << level) * dishes
-            good = look_up(first, (b, c)) > 0.5
-            asked[level, pl.ds(i, 1), :] = jnp.clip(jnp.where(good, second * cols + c, blank), 0, blank)
-            own_rows[level, 0, pl.ds(i, 1), :] = jnp.clip(first * cols + b, 0, blank)
-            own_rows[level, 1, pl.ds(i, 1), :] = jnp.clip(first * cols + c, 0, blank)
+            row = second * cols + c
+            if level == last:
+                row = jnp.where(look_up(a - me * dishes, (b, c)) > 0.5, row, blank)
+            asked[level, pl.ds(i, 1), :] = jnp.clip(row, 0, blank)
 
     def turn(s):
         slot = lax.rem(s, slots)
@@ -165,7 +175,8 @@
         turn(s)
         return 0
 
-    lax.fori_loop(0, 1, turn_step, 0)
+    early, late = steps * 3 // 8, steps * 3 // 4
+    lax.fori_loop(0, early, turn_step, 0)
     pl.semaphore_wait(barrier, len(peers) + len(others))
     ask = [
         remote(asked.at[level], got.at[level], idx_send.at[level], idx_recv.at[level], partner[level])
@@ -173,29 +184,66 @@
     ]
     for copy in ask:
         copy.start()
-    lax.fori_loop(1, steps, turn_step, 0)
-
-    move_own = pltpu.make_async_copy(own_rows, own_smem, move_sem.at[levels])
-    move_own.start()
+    lax.fori_loop(early, late, turn_step, 0)
+
+    def slot_matrix(place):
+        at = lax.broadcasted_iota(jnp.int32, (room, LANES), 0)
+        for i in range(packs):
+            mine = place[i : i + 1, :].astype(jnp.int32)
+            hot[:, pl.ds(i * LANES, LANES)] = jnp.where(at == mine, one, nil).astype(hot.dtype)
+
+    def by_slot(lists):
+        parts = []
+        for rows in lists:
+            flat = blank - jnp.concatenate([rows[i : i + 1, :] for i in range(packs)], 1)
+            parts += [flat // LANES, lax.rem(flat, LANES)]
+        parts.append(jnp.zeros((8 - len(parts), count), jnp.int32))
+        digits = jnp.concatenate(parts, 0).astype(jnp.float32).astype(jnp.bfloat16)
+        moved = lax.dot_general(digits, hot[...], (((1,), (1,)), ((), ())), preferred_element_type=jnp.float32)
+        out = []
+        for i in range(len(lists)):
+            value = moved[2 * i : 2 * i + 1] * LANES + moved[2 * i + 1 : 2 * i + 2]
+            out.append(jnp.clip(blank - value.astype(jnp.int32), 0, blank))
+        return out
+
+    ask[last].wait()
+    for i in range(packs):
+        row = got[last, pl.ds(i, 1), :]
+        good_out[last, pl.ds(i, 1), :] = look_up(row // cols, (lax.rem(row, cols),))
+    good = good_out[last]
+    low = lax.broadcasted_iota(jnp.int32, (LANES, LANES), 0)
+    high = lax.broadcasted_iota(jnp.int32, (LANES, LANES), 1)
+    before = dot(good.astype(jnp.bfloat16), jnp.where(low < high, one, nil).astype(jnp.bfloat16))
+    each = dot(good.astype(jnp.bfloat16), jnp.ones((LANES, LANES), jnp.bfloat16))
+    running, starts = jnp.zeros((1, LANES), jnp.float32), []
+    for i in range(packs):
+        starts.append(running)
+        running = running + each[i : i + 1, :]
+    place = jnp.where(good > 0.5, before + jnp.concatenate(starts, 0), float(2 * count))
+    excess[...] = jnp.where(running > float(room), one, nil)
+    good_out[last] = place
+    slot_matrix(place)
+    (rows,) = by_slot([got[last]])
+    far_rows[...] = jnp.full(far_rows.shape, blank, far_rows.dtype)
+    for i in range(room // LANES):
+        far_rows[pl.ds(i, 1), :] = rows[:, i * LANES : (i + 1) * LANES]
     moves = []
     for level in reversed(range(levels)):
-        ask[level].wait()
-        for i in range(packs):
-            row = got[level, pl.ds(i, 1), :]
-            first, second = row // cols, lax.rem(row, cols)
-            good = look_up(first, (second,)) > 0.5
-            ask_rows[level, pl.ds(i, 1), :] = jnp.clip(jnp.where(good, row, blank), 0, blank)
-        move = pltpu.make_async_copy(ask_rows.at[level], ask_smem.at[level], move_sem.at[level])
-        move.start()
-        moves.append(move)
+        if level < last:
+            ask[level].wait()
+        rows = far_rows if level == last else got.at[level]
+        moves.append(pltpu.make_async_copy(rows, ask_smem.at[level], move_sem.at[level]))
+        moves[-1].start()
+    lax.fori_loop(late, steps, turn_step, 0)
 
     def take(level, start, n):
         unroll = 32
 
         def some(it, _):
+            at = start + it * unroll
+            pack, lane = at // LANES, lax.rem(at, LANES)
             for u in range(unroll):
-                j = start + it * unroll + u
-                bc_send[level, j] = table[ask_smem[level, j // LANES, lax.rem(j, LANES)]]
+                bc_send[level, at + u] = table[ask_smem[level, pack, lane + u]]
             return 0
 
         lax.fori_loop(0, n // unroll, some, 0)
@@ -210,33 +258,78 @@
         )
         for k in range(pieces)
     ]
-    moves[0].wait()
-    for k in range(pieces):
-        take(last, k * FAR, FAR)
-        if k > 0:
-            far[k - 1].start()
     near = [
         remote(bc_send.at[level], bc_recv.at[level], near_send.at[level], near_recv.at[level], partner[level])
         for level in range(last)
     ]
-    for move in moves[1:]:
+    send_good = [
+        remote(good_out.at[level], good_in.at[level], good_send.at[level], good_recv.at[level], partner[level])
+        for level in range(levels)
+    ]
+
+    def look_up_asked(level):
+        for i in range(packs):
+            row = got[level, pl.ds(i, 1), :]
+            good_out[level, pl.ds(i, 1), :] = look_up(row // cols, (lax.rem(row, cols),))
+
+    for move in moves:
         move.wait()
+    take(last, 0, FAR)
+    take(last, FAR, FAR)
+    far[0].start()
+    send_good[last].start()
+    far[1].start()
+    for k in range(2, pieces):
+        take(last, k * FAR, FAR)
+        if k > 2:
+            far[k - 1].start()
     for level in range(last):
+        look_up_asked(level)
         take(level, 0, count)
         if level == 0:
             far[pieces - 1].start()
+        send_good[level].start()
+    goods = []
+    for level in range(last):
+        for i in range(packs):
+            at = level * count + i * LANES
+            a, b, c = [tri[pl.ds(e, 1), pl.ds(at, LANES)] for e in range(3)]
+            goods.append(look_up(a - me * dishes, (b, c)))
+        near[level].start()
+    for level in range(last):
+        send_good[level].wait()
+        for i in range(packs):
+            at = level * count + i * LANES
+            a, b, c = [tri[pl.ds(e, 1), pl.ds(at, LANES)] for e in range(3)]
+            first = a - me * dishes
+            good = goods[level * packs + i] * good_in[level, pl.ds(i, 1), :] > 0.5
+            own_rows[level, 0, pl.ds(i, 1), :] = jnp.clip(jnp.where(good, first * cols + b, blank), 0, blank)
+            own_rows[level, 1, pl.ds(i, 1), :] = jnp.clip(first * cols + c, 0, blank)
+    send_good[last].wait()
+    slot_matrix(good_in[last])
+    lists = [[], []]
+    for i in range(packs):
+        at = last * count + i * LANES
+        a, b, c = [tri[pl.ds(e, 1), pl.ds(at, LANES)] for e in range(3)]
+        first = a - me * dishes
+        lists[0].append(first * cols + b)
+        lists[1].append(first * cols + c)
+    for e, rows in enumerate(by_slot([jnp.concatenate(rows, 0) for rows in lists])):
+        own_rows[last, e] = jnp.full((packs, LANES), blank, jnp.int32)
+        for i in range(room // LANES):
+            own_rows[last, e, pl.ds(i, 1), :] = rows[:, i * LANES : (i + 1) * LANES]
+    move_own = pltpu.make_async_copy(own_rows, own_smem, move_sem.at[levels])
+    move_own.start()
     move_own.wait()
-    for copy in near:
-        copy.start()
-
-    def products(level, n_blocks):
+
+    def products(level, n_blocks, n):
         def some(it, _):
             for s in range(n_blocks):
                 start = (it * n_blocks + s) * block
+                pack, lane = start // LANES, lax.rem(start, LANES)
                 for u in range(block):
-                    j = start + u
                     for e in range(2):
-                        row = table[own_smem[level, e, j // LANES, lax.rem(j, LANES)]]
+                        row = table[own_smem[level, e, pack, lane + u]]
                         pair[s, e, pl.ds(u * kinds, kinds), :] = row
             for s in range(n_blocks):
                 start = pl.multiple_of((it * n_blocks + s) * block, block)
@@ -249,7 +342,7 @@
                     prod[level, 1, c, pl.ds(start, block), :] = a_i * c_r - a_r * c_i
             return 0
 
-        lax.fori_loop(0, count // (n_blocks * block), some, 0)
+        lax.fori_loop(0, n // (n_blocks * block), some, 0)
 
     def bispectra(level, start, n):
         wide = min(2, n // block)
@@ -291,13 +384,12 @@
             )
             sums[0, level, pl.ds(part, 1), pl.ds(pl.multiple_of(start, LANES), n)] = lane_sum[:1]
 
-    products(0, 4 * 32 // block)
-    for level in range(1, levels):
-        products(level, 4 * 32 // block)
+    for level in range(levels):
+        products(level, 4 * 32 // block, room if level == last else count)
     for level in range(last):
         near[level].wait()
         lax.fori_loop(0, count // 256, lambda it, _, level=level: (bispectra(level, it * 256, 256), 0)[1], 0)
-    early = [
+    ahead = [
         remote(sums.at[0, level], sums.at[k, level], sum_send.at[k, level], sum_recv.at[k, level], device)
         for k, device in enumerate(peers, 1)
         for level in range(last)
@@ -306,15 +398,25 @@
         far[k].wait()
         bispectra(last, k * FAR, FAR)
         if k == 0:
-            for copy in early:
+            for copy in ahead:
                 copy.start()
-    copies = list(early)
+    copies = list(ahead)
     for k, device in enumerate(peers, 1):
-        copies.append(remote(sums.at[0, last], sums.at[k, last], sum_send.at[k, last], sum_recv.at[k, last], device))
+        whole = pl.ds(0, room)
+        copies.append(
+            remote(
+                sums.at[0, last, :, whole],
+                sums.at[k, last, :, whole],
+                sum_send.at[k, last],
+                sum_recv.at[k, last],
+                device,
+            )
+        )
         copies[-1].start()
     for c in range(chunks):
         for part in range(3):
             spec_out[c, pl.ds(part, 1), :] = jnp.sum(spec_acc[c, part], 0, keepdims=True)
+        spec_out[c, pl.ds(3, 1), :] = excess[...]
     spread_out = []
     for k, device in enumerate(others, 1):
         spread_out.append(
@@ -331,16 +433,27 @@
         copy.wait()
     bands = channels * groups
     for level in range(levels):
-        total = sums[0, level]
+        n = room if level == last else count
+        total = sums[0, level, :, pl.ds(0, n)]
         for k in range(1, groups):
-            total = total + sums[k, level]
-        means[:, pl.ds(level * count, count)] = total / bands
+            total = total + sums[k, level, :, pl.ds(0, n)]
+        total = total / bands
+        if level == last:
+            parts, rest = [], total
+            for _ in range(3):
+                parts.append(rest.astype(jnp.bfloat16).astype(jnp.float32))
+                rest = rest - parts[-1]
+            parts.append(jnp.zeros((2, room), jnp.float32))
+            moved = dot(jnp.concatenate(parts, 0).astype(jnp.bfloat16), hot[...])
+            total = moved[0:2] + moved[2:4] + moved[4:6]
+        means[:, pl.ds(level * count, count)] = total
     for copy in spread_out:
         copy.wait()
     total = spec_out[me * width // LANES]
     for k in range(1, tiles):
         total = total + spec_recv[k]
-    closure[...] = total[:2] / (1.0 + total[2:3])
+    closure[pl.ds(0, 2), :] = total[:2] / (1.0 + total[2:3])
+    closure[pl.ds(2, 1), :] = total[3:4]
 
 
 def body(visibility, dish_pair_okay, triangles):
@@ -351,7 +464,8 @@
     kinds = 2 * chunks
     packs = TRI_LVL // LANES
     step_rows, slots = 4, 3
-    pieces = TRI_LVL // FAR
+    room = far_room(TRI_LVL)
+    pieces = room // FAR
     width = channels // tiles
     vmem = pl.BlockSpec(memory_space=pltpu.VMEM)
     f32, bf16, i32 = jnp.float32, jnp.bfloat16, jnp.int32
@@ -362,7 +476,7 @@
         out_specs=[vmem, vmem],
         out_shape=[
             jax.ShapeDtypeStruct((2, triangles.shape[1]), f32),
-            jax.ShapeDtypeStruct((2, LANES), f32),
+            jax.ShapeDtypeStruct((3, LANES), f32),
         ],
         scratch_shapes=[
             pltpu.VMEM((dishes * cols + 1, kinds, LANES), bf16),
@@ -371,7 +485,11 @@
             pltpu.VMEM((SIDE, SIDE), bf16),
             pltpu.VMEM((levels, packs, LANES), i32),
             pltpu.VMEM((levels, packs, LANES), i32),
-            pltpu.VMEM((levels, packs, LANES), i32),
+            pltpu.VMEM((levels, packs, LANES), f32),
+            pltpu.VMEM((levels, packs, LANES), f32),
+            pltpu.VMEM((packs, LANES), i32),
+            pltpu.VMEM((room, TRI_LVL), bf16),
+            pltpu.VMEM((1, LANES), f32),
             pltpu.VMEM((levels, 2, packs, LANES), i32),
             pltpu.SMEM((levels, packs, LANES), i32),
             pltpu.SMEM((levels, 2, packs, LANES), i32),
@@ -390,6 +508,8 @@
             dma((levels,)),
             dma((levels,)),
             dma((levels,)),
+            dma((levels,)),
+            dma((levels,)),
             dma((pieces,)),
             dma((pieces,)),
             dma((groups, levels)),
@@ -403,7 +523,41 @@
         name="bispectra",
     )(visibility, dish_pair_okay, triangles)
     at = lax.rem(lax.axis_index("tile") * width, LANES)
-    return (triangle_means, lax.dynamic_slice_in_dim(closure, at, width, 1))
+    return lax.cond(
+        closure[2, 0] > 0.5,
+        lambda: every_row(visibility, dish_pair_okay, triangles),
+        lambda: (triangle_means, lax.dynamic_slice(closure, (0, at), (2, width))),
+    )
+
+
+def every_row(visibility, dish_pair_okay, triangles):
+    _, dishes, cols, channels = visibility.shape
+    levels = triangles.shape[1] // TRI_LVL
+    tiles, groups = lax.axis_size("tile"), lax.axis_size("grp")
+    device = lax.axis_index("tile")
+    table = visibility.reshape(2, dishes * cols, channels)
+    flags = dish_pair_okay.reshape(-1).astype(jnp.float32)
+    means, spectrum = [], 0.0
+    for level in range(levels):
+        pairs = [(i, i ^ 1 << level) for i in range(tiles)]
+        a, b, c = triangles[:, level * TRI_LVL : (level + 1) * TRI_LVL]
+        first = (a - device * dishes) * cols
+        asked = (b - jnp.bitwise_xor(device, 1 << level) * dishes) * cols + c
+        asked = lax.ppermute(asked, "tile", pairs)
+        bc = lax.ppermute(table[:, asked], "tile", pairs).astype(jnp.float32)
+        weight = lax.ppermute(flags[asked], "tile", pairs) * flags[first + b] * flags[first + c]
+        ab, ac = [table[:, first + x].astype(jnp.float32) for x in (b, c)]
+        p_r, p_i = ab[0] * bc[0] - ab[1] * bc[1], ab[0] * bc[1] + ab[1] * bc[0]
+        real = weight[:, None] * (p_r * ac[0] + p_i * ac[1])
+        imag = weight[:, None] * (p_i * ac[0] - p_r * ac[1])
+        norm = jnp.sqrt(real * real + imag * imag)
+        spectrum = spectrum + jnp.stack([x.sum(0) for x in (real, imag, norm)])
+        means.append(jnp.stack([x.sum(1) for x in (real, imag)]))
+    means = lax.psum(jnp.concatenate(means, 1), "grp") / (channels * groups)
+    spectrum = lax.psum(spectrum, "tile")
+    closure = spectrum[:2] / (1.0 + spectrum[2])
+    width = channels // tiles
+    return means, lax.dynamic_slice_in_dim(closure, device * width, width, 1)
 
 
 def solution(mesh):

time: 75.9 us -> 65.3 us (0.86)
  Pallas kernels: 72.4 us -> 60.4 us
    pallas_call x1, Pallas kernels: 72.4 us -> 60.4 us  [body(): pl.pallas_call(functools.partial(mega_kernel, groups=groups, tiles=tiles,...]
    slice x0 -> x1, local copies, waits for them, and re-layouts: none -> 1.19 us  [body(): closure[2, 0] > 0.5]
where the time goes in v1:
time: 65.3 us; the launch traced here: 65 us
  Pallas kernels  60.4 us (92%)
  local copies, waits for them, and re-layouts  3.26 us (5%)
  between operations  1.3 us (2%)
    pallas_call x1, Pallas kernels, body(): pl.pallas_call(functools.partial(mega_kernel, groups=groups, tiles=tiles,...  60.4 us
    unnamed x3, local copies, waits for them, and re-layouts  1.33 us

profile of v1, /device:TPU:0, one launch (start us, length us, event | category | flops | bytes accessed | tf_op | source)
XLA Modules:
  0.0 65.0 jit_solution(17150732434582791087)
XLA Ops:
  0.6 60.4 %bispectra.1 = (f32[2,2048]{1,0:T(2,128)}, f32[3,128]{1,0:T(4,128)}) custom-call(bf16[2,32,512,512]{3,2,1,0:T(8,128)(2,1)} %vis.1, s32[32,512]{1,0:T(8,128)} %okay.1, s32[3,2048]{1,0:T(4,128)} %tri.1), custom_call_target="tpu_custom_call" | custom-call | tf_op jit(solution)/shard_map/bispectra/pallas_call | solution.py:473
  61.1 1.2 %slice.65 = f32[1,1]{1,0:T(1,128)} slice(f32[3,128]{1,0:T(4,128)} %get-tuple-element.36), slice={[2:3], [0:1]} | slice | bytes 8 | tf_op jit(solution)/shard_map/slice | solution.py:527
  62.9 0.8 %conditional.1 = (f32[2,2048]{1,0:T(2,128)}, f32[2,32]{1,0:T(2,128)S(1)}) conditional(s32[]{:T(128)} %bitcast.32, (s32[]{:T(128)}, f32[3,128]{1,0:T(4,128)}, f32[2,2048]{1,0:T(2,128)}) %tuple.20, (s32[32,512]{1,0:T(8,128)}, s32[3,2048]{1,0:T(4,128)}, bf16[2,32,512,512]{3,2,1,0:T(8,128)(2,1)}) %tuple.21), branch_computations={%region_0.0_spmd, %region_1.0_spmd} | conditional | flops 29442632 | bytes 273390912 | solution.py:526
  62.9 0.7 %constant_dynamic-slice_fusion = f32[2,32]{1,0:T(2,128)S(1)} fusion(f32[3,128]{1,0:T(4,128)} %get-tuple-element.27, s32[]{:T(128)S(6)} %select_n.50), kind=kLoop, calls=%fused_computation.12 | loop fusion | bytes 516 | tf_op jit(solution)/shard_map/cond/branch_0_fun/dynamic_slice | solution.py:529
  63.7 0.0 copy-start.4
  63.7 1.3 %copy.47 = f32[2,2048]{1,0:T(2,128)} copy(f32[2,2048]{1,0:T(2,128)} %get-tuple-element.78) | data formatting | bytes 32768
  65.0 0.0 copy-done.4
Async XLA Ops:
  63.7 1.3 %copy-start.4 = (f32[2,32]{1,0:T(2,128)}, f32[2,32]{1,0:T(2,128)S(1)}, u32[]{:S(2)}) copy-start(f32[2,32]{1,0:T(2,128)S(1)} %get-tuple-element.79) | copy-start | bytes 772

commit v2 on v1

--- a/solution.py
+++ b/solution.py
@@ -11,6 +11,8 @@
 LANES = 128
 SIDE = 256
 FAR = 128
+FIRST = 256
+EARLY = 1
 MESH = pl.DeviceIdType.MESH
 
 
@@ -175,7 +177,7 @@
         turn(s)
         return 0
 
-    early, late = steps * 3 // 8, steps * 3 // 4
+    early, late, ready = EARLY, max(EARLY, steps * 3 // 8), steps // 2
     lax.fori_loop(0, early, turn_step, 0)
     pl.semaphore_wait(barrier, len(peers) + len(others))
     ask = [
@@ -211,16 +213,33 @@
         row = got[last, pl.ds(i, 1), :]
         good_out[last, pl.ds(i, 1), :] = look_up(row // cols, (lax.rem(row, cols),))
     good = good_out[last]
+    antenna = got[last] // cols
     low = lax.broadcasted_iota(jnp.int32, (LANES, LANES), 0)
     high = lax.broadcasted_iota(jnp.int32, (LANES, LANES), 1)
-    before = dot(good.astype(jnp.bfloat16), jnp.where(low < high, one, nil).astype(jnp.bfloat16))
-    each = dot(good.astype(jnp.bfloat16), jnp.ones((LANES, LANES), jnp.bfloat16))
-    running, starts = jnp.zeros((1, LANES), jnp.float32), []
+    ahead_of = jnp.where(low < high, one, nil).astype(jnp.bfloat16)
+    every = jnp.ones((LANES, LANES), jnp.bfloat16)
+    number = lax.broadcasted_iota(jnp.int32, (dishes, LANES), 0)
+    running, seen = jnp.zeros((dishes, LANES), jnp.float32), []
     for i in range(packs):
-        starts.append(running)
-        running = running + each[i : i + 1, :]
-    place = jnp.where(good > 0.5, before + jnp.concatenate(starts, 0), float(2 * count))
-    excess[...] = jnp.where(running > float(room), one, nil)
+        mine = jnp.where(number == antenna[i : i + 1, :], good[i : i + 1, :], 0.0)
+        mark = mine.astype(jnp.bfloat16)
+        seen.append((mine, running + dot(mark, ahead_of)))
+        running = running + dot(mark, every)
+    row = lax.broadcasted_iota(jnp.int32, (dishes, dishes), 0)
+    column = lax.broadcasted_iota(jnp.int32, (dishes, dishes), 1)
+    offset = lax.dot_general(
+        jnp.where(column < row, one, nil),
+        running,
+        (((1,), (0,)), ((), ())),
+        precision=lax.Precision.HIGHEST,
+        preferred_element_type=jnp.float32,
+    )
+    place = jnp.concatenate([jnp.sum(mine * (at + offset), 0, keepdims=True) for mine, at in seen], 0)
+    place = jnp.where(good > 0.5, place, float(2 * count))
+    used = jnp.sum(running, 0, keepdims=True)
+    soon = jnp.sum(jnp.where(number < ready * step_rows, running, 0.0), 0, keepdims=True)
+    fits = (used <= float(room)) & (soon >= jnp.minimum(used, float(FIRST)))
+    excess[...] = jnp.where(fits, nil, one)
     good_out[last] = place
     slot_matrix(place)
     (rows,) = by_slot([got[last]])
@@ -234,7 +253,7 @@
         rows = far_rows if level == last else got.at[level]
         moves.append(pltpu.make_async_copy(rows, ask_smem.at[level], move_sem.at[level]))
         moves[-1].start()
-    lax.fori_loop(late, steps, turn_step, 0)
+    lax.fori_loop(late, ready, turn_step, 0)
 
     def take(level, start, n):
         unroll = 32
@@ -274,14 +293,16 @@
 
     for move in moves:
         move.wait()
-    take(last, 0, FAR)
-    take(last, FAR, FAR)
-    far[0].start()
-    send_good[last].start()
-    far[1].start()
-    for k in range(2, pieces):
+    for k in range(FIRST // FAR):
         take(last, k * FAR, FAR)
-        if k > 2:
+    for k in range(FIRST // FAR):
+        far[k].start()
+        if k == 0:
+            send_good[last].start()
+    lax.fori_loop(ready, steps, turn_step, 0)
+    for k in range(FIRST // FAR, pieces):
+        take(last, k * FAR, FAR)
+        if k > FIRST // FAR:
             far[k - 1].start()
     for level in range(last):
         look_up_asked(level)

time: 65.3 us -> 60.3 us (0.923)
  Pallas kernels: 60.4 us -> 55.4 us
    pallas_call x1, Pallas kernels: 60.4 us -> 55.4 us  [body(): pl.pallas_call(functools.partial(mega_kernel, groups=groups, tiles=tiles,...]
where the time goes in v2:
time: 60.3 us; the launch traced here: 60 us
  Pallas kernels  55.4 us (92%)
  local copies, waits for them, and re-layouts  3.26 us (5%)
  between operations  1.3 us (2%)
    pallas_call x1, Pallas kernels, body(): pl.pallas_call(functools.partial(mega_kernel, groups=groups, tiles=tiles,...  55.4 us
    unnamed x3, local copies, waits for them, and re-layouts  1.33 us

profile of v2, /device:TPU:0, one launch (start us, length us, event | category | flops | bytes accessed | tf_op | source)
XLA Modules:
  0.0 60.0 jit_solution(11086996884380226123)
XLA Ops:
  0.6 55.4 %bispectra.1 = (f32[2,2048]{1,0:T(2,128)}, f32[3,128]{1,0:T(4,128)}) custom-call(bf16[2,32,512,512]{3,2,1,0:T(8,128)(2,1)} %vis.1, s32[32,512]{1,0:T(8,128)} %okay.1, s32[3,2048]{1,0:T(4,128)} %tri.1), custom_call_target="tpu_custom_call" | custom-call | tf_op jit(solution)/shard_map/bispectra/pallas_call | solution.py:494
  56.0 1.2 %slice.65 = f32[1,1]{1,0:T(1,128)} slice(f32[3,128]{1,0:T(4,128)} %get-tuple-element.36), slice={[2:3], [0:1]} | slice | bytes 8 | tf_op jit(solution)/shard_map/slice | solution.py:548
  57.9 0.8 %conditional.1 = (f32[2,2048]{1,0:T(2,128)}, f32[2,32]{1,0:T(2,128)S(1)}) conditional(s32[]{:T(128)} %bitcast.32, (s32[]{:T(128)}, f32[3,128]{1,0:T(4,128)}, f32[2,2048]{1,0:T(2,128)}) %tuple.20, (s32[32,512]{1,0:T(8,128)}, s32[3,2048]{1,0:T(4,128)}, bf16[2,32,512,512]{3,2,1,0:T(8,128)(2,1)}) %tuple.21), branch_computations={%region_0.0_spmd, %region_1.0_spmd} | conditional | flops 29442632 | bytes 273390912 | solution.py:547
  57.9 0.7 %constant_dynamic-slice_fusion = f32[2,32]{1,0:T(2,128)S(1)} fusion(f32[3,128]{1,0:T(4,128)} %get-tuple-element.27, s32[]{:T(128)S(6)} %select_n.50), kind=kLoop, calls=%fused_computation.12 | loop fusion | bytes 516 | tf_op jit(solution)/shard_map/cond/branch_0_fun/dynamic_slice | solution.py:550
  58.6 0.0 copy-start.4
  58.7 1.3 %copy.47 = f32[2,2048]{1,0:T(2,128)} copy(f32[2,2048]{1,0:T(2,128)} %get-tuple-element.78) | data formatting | bytes 32768
  60.0 0.0 copy-done.4
Async XLA Ops:
  58.6 1.3 %copy-start.4 = (f32[2,32]{1,0:T(2,128)}, f32[2,32]{1,0:T(2,128)S(1)}, u32[]{:S(2)}) copy-start(f32[2,32]{1,0:T(2,128)S(1)} %get-tuple-element.79) | copy-start | bytes 772

commit v3 on v2

--- a/solution.py
+++ b/solution.py
@@ -37,6 +37,7 @@
     tri,
     means,
     closure,
+    missed,
     table,
     ring,
     spread,
@@ -177,7 +178,8 @@
         turn(s)
         return 0
 
-    early, late, ready = EARLY, max(EARLY, steps * 3 // 8), steps // 2
+    early, late = EARLY, max(EARLY, steps * 3 // 8)
+    ready = [min(steps, late + k) for k in range(FIRST // FAR)]
     lax.fori_loop(0, early, turn_step, 0)
     pl.semaphore_wait(barrier, len(peers) + len(others))
     ask = [
@@ -237,8 +239,10 @@
     place = jnp.concatenate([jnp.sum(mine * (at + offset), 0, keepdims=True) for mine, at in seen], 0)
     place = jnp.where(good > 0.5, place, float(2 * count))
     used = jnp.sum(running, 0, keepdims=True)
-    soon = jnp.sum(jnp.where(number < ready * step_rows, running, 0.0), 0, keepdims=True)
-    fits = (used <= float(room)) & (soon >= jnp.minimum(used, float(FIRST)))
+    fits = used <= float(room)
+    for k, done in enumerate(ready, 1):
+        soon = jnp.sum(jnp.where(number < done * step_rows, running, 0.0), 0, keepdims=True)
+        fits = fits & (soon >= jnp.minimum(used, float(k * FAR)))
     excess[...] = jnp.where(fits, nil, one)
     good_out[last] = place
     slot_matrix(place)
@@ -253,7 +257,6 @@
         rows = far_rows if level == last else got.at[level]
         moves.append(pltpu.make_async_copy(rows, ask_smem.at[level], move_sem.at[level]))
         moves[-1].start()
-    lax.fori_loop(late, ready, turn_step, 0)
 
     def take(level, start, n):
         unroll = 32
@@ -293,13 +296,15 @@
 
     for move in moves:
         move.wait()
-    for k in range(FIRST // FAR):
+    at = late
+    for k, done in enumerate(ready):
+        lax.fori_loop(at, done, turn_step, 0)
+        at = done
         take(last, k * FAR, FAR)
-    for k in range(FIRST // FAR):
         far[k].start()
         if k == 0:
             send_good[last].start()
-    lax.fori_loop(ready, steps, turn_step, 0)
+    lax.fori_loop(at, steps, turn_step, 0)
     for k in range(FIRST // FAR, pieces):
         take(last, k * FAR, FAR)
         if k > FIRST // FAR:
@@ -473,8 +478,8 @@
     total = spec_out[me * width // LANES]
     for k in range(1, tiles):
         total = total + spec_recv[k]
-    closure[pl.ds(0, 2), :] = total[:2] / (1.0 + total[2:3])
-    closure[pl.ds(2, 1), :] = total[3:4]
+    closure[...] = total[:2] / (1.0 + total[2:3])
+    missed[0] = jnp.max(total[3:4]).astype(jnp.int32)
 
 
 def body(visibility, dish_pair_okay, triangles):
@@ -491,13 +496,14 @@
     vmem = pl.BlockSpec(memory_space=pltpu.VMEM)
     f32, bf16, i32 = jnp.float32, jnp.bfloat16, jnp.int32
     dma = pltpu.SemaphoreType.DMA
-    triangle_means, closure = pl.pallas_call(
+    triangle_means, closure, missed = pl.pallas_call(
         functools.partial(mega_kernel, groups=groups, tiles=tiles, levels=levels, step_rows=step_rows),
         in_specs=[pl.BlockSpec(memory_space=pl.ANY), vmem, vmem],
-        out_specs=[vmem, vmem],
+        out_specs=[vmem, vmem, pl.BlockSpec(memory_space=pltpu.SMEM)],
         out_shape=[
             jax.ShapeDtypeStruct((2, triangles.shape[1]), f32),
-            jax.ShapeDtypeStruct((3, LANES), f32),
+            jax.ShapeDtypeStruct((2, LANES), f32),
+            jax.ShapeDtypeStruct((1,), i32),
         ],
         scratch_shapes=[
             pltpu.VMEM((dishes * cols + 1, kinds, LANES), bf16),
@@ -545,7 +551,7 @@
     )(visibility, dish_pair_okay, triangles)
     at = lax.rem(lax.axis_index("tile") * width, LANES)
     return lax.cond(
-        closure[2, 0] > 0.5,
+        missed[0] > 0,
         lambda: every_row(visibility, dish_pair_okay, triangles),
         lambda: (triangle_means, lax.dynamic_slice(closure, (0, at), (2, width))),
     )

time: 60.3 us -> 58 us (0.962)
  local copies, waits for them, and re-layouts: 3.26 us -> 2.07 us
  Pallas kernels: 55.4 us -> 54.3 us
    slice x1 -> x0, local copies, waits for them, and re-layouts: 1.19 us -> none  [body(): closure[2, 0] > 0.5]
    pallas_call x1, Pallas kernels: 55.4 us -> 54.3 us  [body(): pl.pallas_call(functools.partial(mega_kernel, groups=groups, tiles=tiles,...]
where the time goes in v3:
time: 58 us; the launch traced here: 57.7 us
  Pallas kernels  54.3 us (94%)
  local copies, waits for them, and re-layouts  2.07 us (4%)
  between operations  1.33 us (2%)
    pallas_call x1, Pallas kernels, body(): pl.pallas_call(functools.partial(mega_kernel, groups=groups, tiles=tiles,...  54.3 us
    unnamed x3, local copies, waits for them, and re-layouts  1.33 us

profile of v3, /device:TPU:0, one launch (start us, length us, event | category | flops | bytes accessed | tf_op | source)
XLA Modules:
  0.0 57.7 jit_solution(5604616934841380464)
XLA Ops:
  0.6 54.3 %bispectra.1 = (f32[2,2048]{1,0:T(2,128)}, f32[2,128]{1,0:T(2,128)}, s32[1]{0:T(128)}) custom-call(bf16[2,32,512,512]{3,2,1,0:T(8,128)(2,1)} %vis.1, s32[32,512]{1,0:T(8,128)} %okay.1, s32[3,2048]{1,0:T(4,128)} %tri.1), custom_call_target="tpu_custom_call" | custom-call | tf_op jit(solution)/shard_map/bispectra/pallas_call | solution.py:499
  55.6 0.8 %conditional.1 = (f32[2,2048]{1,0:T(2,128)}, f32[2,32]{1,0:T(2,128)S(1)}) conditional(s32[]{:T(128)} %bitcast.32, (s32[]{:T(128)}, f32[2,128]{1,0:T(2,128)}, f32[2,2048]{1,0:T(2,128)}) %tuple.19, (s32[32,512]{1,0:T(8,128)}, s32[3,2048]{1,0:T(4,128)}, bf16[2,32,512,512]{3,2,1,0:T(8,128)(2,1)}) %tuple.20), branch_computations={%region_0.0_spmd, %region_1.0_spmd} | conditional | flops 29442632 | bytes 273390912 | solution.py:553
  55.7 0.7 %constant_dynamic-slice_fusion = f32[2,32]{1,0:T(2,128)S(1)} fusion(f32[2,128]{1,0:T(2,128)} %get-tuple-element.27, s32[]{:T(128)S(6)} %select_n.50), kind=kLoop, calls=%fused_computation.12 | loop fusion | bytes 516 | tf_op jit(solution)/shard_map/cond/branch_0_fun/dynamic_slice | solution.py:556
  56.4 0.0 copy-start.4
  56.4 1.3 %copy.47 = f32[2,2048]{1,0:T(2,128)} copy(f32[2,2048]{1,0:T(2,128)} %get-tuple-element.80) | data formatting | bytes 32768
  57.7 0.0 copy-done.4
Async XLA Ops:
  56.4 1.3 %copy-start.4 = (f32[2,32]{1,0:T(2,128)}, f32[2,32]{1,0:T(2,128)S(1)}, u32[]{:S(2)}) copy-start(f32[2,32]{1,0:T(2,128)S(1)} %get-tuple-element.81) | copy-start | bytes 772
